TPU v7x, 128 devices: a whole 4x4x4 slice. The times are simulated.
128 devices in a mesh: dp: 16 (over y, x), tensor: 8 (over z, core).
Axes of the slice: x: 4, y: 4, z: 4, core: 2. Of those that a mesh axis runs over, the one named last changes fastest.
Arguments:
- tokens: bfloat16 [8192, 3584], P('dp'), may hold values from -6 to 6
- gate_weight: bfloat16 [3584, 10240], P(None, 'tensor'), may hold values from -0.09375 to 0.09375
- up_act: bfloat16 [8192, 10240], P('dp', 'tensor'), may hold values from -6 to 6
- hidden_cot: bfloat16 [8192, 10240], P('dp', 'tensor'), may hold values from -6 to 6
- lag_grads: bfloat16 [16, 3584, 10240], P('dp', None, 'tensor'), may hold values from -8 to 8, as said below
- skip_mask: int32 [16], P('dp'), may hold values 0 or 1
- aggregate: float32 [3584, 10240], P('dp', 'tensor'), may hold values from -3 to 3
Outputs:
- new_aggregate: float32 [3584, 10240], P('dp', 'tensor')
- input_grad: bfloat16 [8192, 3584], P('dp', 'tensor')
- change_rms: float32 [16], P('dp')
Inputs may be any that keep to these rules, and one draw needn't show every extreme that they name: `lag_grads`: real-valued.
All inputs are finite; a program needn't handle non-finite values. No bound on the sum of `skip_mask` on one device may be relied on, other than what follows from the above.
Results may differ from a plain program's by a relative error of at most 0.014.
Values may be sent and summed in bfloat16 or wider, within the bound.
No kernel may reach another device: no remote copies, remote signals or barrier semaphores. Data moves between devices by JAX's collectives and lax.ppermute only.
A program may use at most 128 MiB of HBM per device.

v0:
```python
import jax
import jax.numpy as jnp
from jax import lax
from jax.sharding import Mesh
from jax.sharding import PartitionSpec as P

D = 3584
FF = 10240
TOK_DEV = 512
TENSOR = ("tensor_0", "tensor_1")


clip_level = 0.1


def split_up(value, dim, size):
    shape = value.shape
    parts = value.reshape(*shape[:dim], size, shape[dim] // size, *shape[dim + 1 :])
    return jnp.moveaxis(parts, dim, 0)


def sent_and_summed(value, axis, dim):
    parts = split_up(value, dim, lax.axis_size(axis))
    arrived = lax.all_to_all(parts, axis, split_axis=0, concat_axis=0, tiled=True)
    return arrived.astype(jnp.float32).sum(axis=0)


def sum_by_axis(value, axes, dim):
    far, near = axes
    parts = split_up(value, dim, lax.axis_size(far))
    nearer = sent_and_summed(parts, near, dim + 1)
    arrived = lax.all_to_all(
        nearer.astype(jnp.bfloat16), far, split_axis=0, concat_axis=0, tiled=True
    )
    return arrived.astype(jnp.float32).sum(axis=0)


def from_everyone(value, axis):
    size = lax.axis_size(axis)
    return lax.all_to_all(
        jnp.broadcast_to(value[None], (size, *value.shape)), axis, 0, 0, tiled=True
    )


def of_everyone(value, axis):
    everything = from_everyone(value, axis)
    return jnp.sum(everything, axis=0)


def body(tokens, gate_weight, up_act, hidden_cot, lag_grads, skip_mask, aggregate):
    gate = jnp.dot(tokens, gate_weight, preferred_element_type=jnp.float32)
    sig = jax.nn.sigmoid(gate)
    d_gate = (
        hidden_cot.astype(jnp.float32)
        * up_act.astype(jnp.float32)
        * sig
        * (1.0 + gate * (1.0 - sig))
    ).astype(jnp.bfloat16)
    partial_input = lax.dot_general(
        d_gate, gate_weight, (((1,), (1,)), ((), ())), preferred_element_type=jnp.float32
    )
    input_grad = sum_by_axis(
        partial_input.astype(jnp.bfloat16), ("tensor_0", "tensor_1"), 1
    ).astype(jnp.bfloat16)
    inverse = 1.0 / TOK_DEV
    lagged = lag_grads[0]
    grad = (
        lax.dot_general(
            tokens, d_gate, (((0,), (0,)), ((), ())), preferred_element_type=jnp.float32
        )
        * inverse
    )
    change = grad - lagged.astype(jnp.float32)
    total_sq = of_everyone(jnp.sum(change * change), TENSOR)
    rms = jnp.sqrt(total_sq / (D * FF) + 1e-06)
    factor = skip_mask[0].astype(jnp.float32) * jnp.minimum(1.0, clip_level / rms)
    sent = (factor * change).astype(jnp.bfloat16)
    summed = lax.psum_scatter(sent, "dp", scatter_dimension=0, tiled=True).astype(jnp.float32)
    return (aggregate + summed, input_grad, rms.reshape(1))


def solution(mesh):
    finer = Mesh(mesh.devices.reshape(mesh.shape["dp"], 4, 2), ("dp", "tensor_0", "tensor_1"))
    placed = (
        P("dp", None),
        P(None, TENSOR),
        P("dp", TENSOR),
        P("dp", TENSOR),
        P("dp", None, TENSOR),
        P("dp"),
        P("dp", TENSOR),
    )
    return jax.shard_map(
        body,
        mesh=finer,
        in_specs=placed,
        out_specs=(P("dp", TENSOR), P("dp", TENSOR), P("dp")),
        check_vma=False,
    )
```

profile of v0, /device:TPU:0, one launch (start us, length us, event | category | flops | bytes accessed | tf_op | source)
XLA Modules:
  0.0 178.9 jit_solution(4380383151770798053)
XLA Ops:
  7.2 12.8 %copy.29 = bf16[1,3584,1280]{1,2,0:T(8,128)(2,1)} copy(bf16[1,3584,1280]{2,1,0:T(8,128)(2,1)} %param.11) | data formatting | bytes 18350080 | tf_op args[4]
  20.0 9.7 %fusion.4 = f32[512,1280]{1,0:T(8,128)S(1)} fusion(bf16[512,3584]{1,0:T(8,128)(2,1)} %param.7, bf16[3584,1280]{1,0:T(8,128)(2,1)} %param.8), kind=kOutput, calls=%fused_computation.12 | convolution fusion | flops 4697620480 | bytes 15466496 | tf_op jit(solution)/shard_map/dot_general | solution.py:51
  29.8 12.2 %multiply_reduce_fusion = (f32[]{:T(128)}, f32[3584,1280]{0,1:T(8,128)}) fusion(bf16[1,3584,1280]{1,2,0:T(8,128)(2,1)S(1)} %copy-done, bf16[512,3584]{1,0:T(8,128)(2,1)S(1)} %copy-done.1, f32[512,1280]{1,0:T(8,128)S(1)} %fusion.4, bf16[512,1280]{1,0:T(8,128)(2,1)S(1)} %copy-done.2, bf16[512,1280]{1,0:T(8,128)(2,1)S(1)} %copy-done.3), kind=kOutput, calls=%fused_computation.3 | convolution fusion | flops 4728422400 | bytes 36438020 | tf_op jit(solution)/shard_map/dot_general | solution.py:68
  42.0 1.2 broadcast_in_dim.2
  43.2 5.4 %all-to-all-start = ((f32[8,1,1]{2,1,0:T(1,128)}), f32[8,1,1]{2,1,0:T(1,128)S(1)}, u32[]{:S(2)}, u32[]{:S(2)}) async-start(f32[8,1,1]{2,1,0:T(1,128)} %broadcast_in_dim.2), calls=%async_computation | async-start | bytes 8192 | tf_op jit(solution)/shard_map/all_to_all | solution.py:40
  48.7 0.2 reduce-scatter.4.cloned.1.call-start
  49.6 4.3 %all-to-all-done = f32[8,1,1]{2,1,0:T(1,128)S(1)} async-done(((f32[8,1,1]{2,1,0:T(1,128)}), f32[8,1,1]{2,1,0:T(1,128)S(1)}, u32[]{:S(2)}, u32[]{:S(2)}) %all-to-all-start) | async-done | bytes 64 | tf_op jit(solution)/shard_map/all_to_all | solution.py:40
  53.9 0.6 reduce_sum.43
  55.3 11.1 %multiply_convert_fusion = bf16[3584,1280]{0,1:T(8,128)(2,1)} fusion(f32[3584,1280]{0,1:T(8,128)} %get-tuple-element.19, f32[]{:T(128)S(6)} %mul.41), kind=kLoop, calls=%fused_computation.2 | loop fusion | flops 9175040 | bytes 27525124 | tf_op jit(solution)/shard_map/convert_element_type | solution.py:77
  66.3 12.8 %copy.37 = bf16[3584,1280]{1,0:T(8,128)(2,1)} copy(bf16[3584,1280]{0,1:T(8,128)(2,1)} %multiply_convert_fusion) | data formatting | bytes 18350080
  79.1 0.0 reduce-scatter.4.cloned.1.call-update
  79.1 11.6 %convolution_convert_fusion = bf16[512,3584]{1,0:T(8,128)(2,1)} fusion(bf16[3584,1280]{1,0:T(8,128)(2,1)} %param.8, f32[512,1280]{1,0:T(8,128)} %copy-done.4, bf16[512,1280]{1,0:T(8,128)(2,1)S(1)} %copy-done.2, bf16[512,1280]{1,0:T(8,128)(2,1)S(1)} %copy-done.3), kind=kOutput, calls=%fused_computation.4 | convolution fusion | flops 4707319808 | bytes 18087936 | tf_op jit(solution)/shard_map/dot_general | solution.py:59
  90.7 5.9 %copy.36 = bf16[512,3584]{0,1:T(8,128)(2,1)} copy(bf16[512,3584]{1,0:T(8,128)(2,1)} %convolution_convert_fusion) | data formatting | bytes 7340032 | tf_op jit(solution)/shard_map/reshape | solution.py:18
  96.6 2.3 %copy.33 = bf16[2,4,512,448]{2,3,1,0:T(8,128)(2,1)S(1)} copy(bf16[2,4,512,448]{2,3,0,1:T(8,128)(2,1)} %bitcast.19) | data formatting | bytes 7340032 | tf_op jit(solution)/shard_map/transpose | solution.py:19
  98.9 7.7 %all_to_all.16 = bf16[2,4,512,448]{2,3,1,0:T(8,128)(2,1)} all-to-all(bf16[2,4,512,448]{2,3,1,0:T(8,128)(2,1)S(1)} %copy.33), channel_id=1, replica_groups=mesh['dp'=16,'tensor_0'=4,'tensor_1'=2] {'tensor_1'}, dimensions={0} | all-to-all | bytes 7340032 | tf_op jit(solution)/shard_map/all_to_all | solution.py:24
  106.6 4.6 %reduce_sum.44 = bf16[4,512,448]{1,2,0:T(8,128)(2,1)} reduce(bf16[2,4,512,448]{2,3,1,0:T(8,128)(2,1)} %all_to_all.16, bf16[]{:T(256)} %constant.16.clone.1), dimensions={0}, to_apply=%region_3.0 | reduce | flops 917504 | bytes 5505026 | tf_op jit(solution)/shard_map/reduce_sum | solution.py:25
  111.2 3.6 %all-to-all-start.2 = ((bf16[4,512,448]{1,2,0:T(8,128)(2,1)}), bf16[4,512,448]{1,2,0:T(8,128)(2,1)S(1)}, u32[]{:S(2)}, u32[]{:S(2)}) async-start(bf16[4,512,448]{1,2,0:T(8,128)(2,1)} %reduce_sum.44), calls=%async_computation.2 | async-start | bytes 3670016 | tf_op jit(solution)/shard_map/all_to_all | solution.py:32
  114.8 1.7 copy.31
  116.4 22.4 %all-to-all-done.2 = bf16[4,512,448]{1,2,0:T(8,128)(2,1)S(1)} async-done(((bf16[4,512,448]{1,2,0:T(8,128)(2,1)}), bf16[4,512,448]{1,2,0:T(8,128)(2,1)S(1)}, u32[]{:S(2)}, u32[]{:S(2)}) %all-to-all-start.2) | async-done | bytes 1835040 | tf_op jit(solution)/shard_map/all_to_all | solution.py:32
  138.8 1.2 reduce_sum.45
  140.0 26.2 %reduce-scatter.4.cloned.1.call-done = bf16[224,1280]{1,0:T(8,128)(2,1)} async-done(((bf16[3584,1280]{1,0:T(8,128)(2,1)}), bf16[224,1280]{1,0:T(8,128)(2,1)}) %reduce-scatter.4.cloned.1.call-update) | async-done | bytes 573456
  166.1 2.1 %copy.38 = bf16[224,1280]{0,1:T(8,128)(2,1)} copy(bf16[224,1280]{1,0:T(8,128)(2,1)} %reduce-scatter.4.cloned.1.call-done) | data formatting | bytes 1146880
  168.3 1.2 convert_add_fusion
  169.5 1.4 copy.35
  (10 shorter events, 0.0 us)
Async XLA Ops:
  20.0 9.8 %copy-start = (bf16[1,3584,1280]{1,2,0:T(8,128)(2,1)S(1)}, bf16[1,3584,1280]{1,2,0:T(8,128)(2,1)}, u32[]{:S(2)}) copy-start(bf16[1,3584,1280]{1,2,0:T(8,128)(2,1)} %copy.29) | copy-start | bytes 27525124
  20.0 9.8 %copy-start.1 = (bf16[512,3584]{1,0:T(8,128)(2,1)S(1)}, bf16[512,3584]{1,0:T(8,128)(2,1)}, u32[]{:S(2)}) copy-start(bf16[512,3584]{1,0:T(8,128)(2,1)} %param.7) | copy-start | bytes 11010052
  20.0 9.8 %copy-start.2 = (bf16[512,1280]{1,0:T(8,128)(2,1)S(1)}, bf16[512,1280]{1,0:T(8,128)(2,1)}, u32[]{:S(2)}) copy-start(bf16[512,1280]{1,0:T(8,128)(2,1)} %param.9) | copy-start | bytes 3932164
  20.0 9.8 %copy-start.3 = (bf16[512,1280]{1,0:T(8,128)(2,1)S(1)}, bf16[512,1280]{1,0:T(8,128)(2,1)}, u32[]{:S(2)}) copy-start(bf16[512,1280]{1,0:T(8,128)(2,1)} %param.10) | copy-start | bytes 3932164
  29.8 12.2 %copy-start.4 = (f32[512,1280]{1,0:T(8,128)}, f32[512,1280]{1,0:T(8,128)S(1)}, u32[]{:S(2)}) copy-start(f32[512,1280]{1,0:T(8,128)S(1)} %fusion.4) | copy-start | bytes 7864324
  43.2 10.7 %all-to-all-start = ((f32[8,1,1]{2,1,0:T(1,128)}), f32[8,1,1]{2,1,0:T(1,128)S(1)}, u32[]{:S(2)}, u32[]{:S(2)}) async-start(f32[8,1,1]{2,1,0:T(1,128)} %broadcast_in_dim.2), calls=%async_computation | async-start | bytes 8192 | tf_op jit(solution)/shard_map/all_to_all | solution.py:40
  48.7 117.5 %reduce-scatter.4.cloned.1.call-start = ((), (), s32[]{:S(2)}) async-start(), calls=%async_computation.4 | async-start | bytes 9748480
  111.2 27.7 %all-to-all-start.2 = ((bf16[4,512,448]{1,2,0:T(8,128)(2,1)}), bf16[4,512,448]{1,2,0:T(8,128)(2,1)S(1)}, u32[]{:S(2)}, u32[]{:S(2)}) async-start(bf16[4,512,448]{1,2,0:T(8,128)(2,1)} %reduce_sum.44), calls=%async_computation.2 | async-start | bytes 3670016 | tf_op jit(solution)/shard_map/all_to_all | solution.py:32
Sparse Core Ops, SparseCore 0:
  79.2 86.8 reduce-scatter.3
where the time goes:
time: 180 us; the launch traced here: 179 us
  waiting for transfers between devices  52.9 us (29%)
  local copies, waits for them, and re-layouts  40.2 us (22%)
  matrix products  33.5 us (19%)
  other arithmetic  18.7 us (10%)
  between operations  16.6 us (9%)
  starting transfers between devices  9.25 us (5%)
  blocking collectives  7.7 us (4%)
    unnamed x15, local copies, waits for them, and re-layouts  30.8 us
    unnamed x2, waiting for transfers between devices  26.2 us
    all_to_all x1, waiting for transfers between devices, sum_by_axis(): lax.all_to_all(nearer.astype(jnp.bfloat16), far, split_axis=0, concat_axi...  22.4 us
    dot_general x1, matrix products, body(): lax.dot_general(tokens, d_gate, (((0,), (0,)), ((), ())), preferred_eleme...  12.2 us
    dot_general x1, matrix products, body(): lax.dot_general(d_gate, gate_weight, (((1,), (1,)), ((), ())), preferred_...  11.6 us
    convert_element_type x1, other arithmetic, body(): sent = (factor * change).astype(jnp.bfloat16)  11.1 us
    dot_general x1, matrix products, body(): gate = jnp.dot(tokens, gate_weight, preferred_element_type=jnp.float32)  9.75 us
    all_to_all x1, blocking collectives, sent_and_summed(): lax.all_to_all(parts, axis, split_axis=0, concat_axis=0, tiled=True)  7.7 us
  transfers between devices with their start and end apart: 3, of which 3 were waited for; matrix products, arithmetic and copies ran while one was open for 15% of the time, Pallas kernels for 0%

commit v1 on v0

v1 whole, which is shorter than its diff:
```python
import jax
import jax.numpy as jnp
from jax import lax
from jax.experimental import pallas as pl
from jax.experimental.pallas import tpu as pltpu
from jax.sharding import Mesh
from jax.sharding import PartitionSpec as P

D = 3584
FF = 10240
TOK = 512
COLS = 1280
HALF = 640
CHUNK = 256
BLK = 224
SUB = 112
INB = 448
CLIP = 0.1
MIB = 1024 * 1024
TENSOR = ("z", "c")
EVEN = [(0, 1), (1, 0), (2, 3), (3, 2)]
ODD = [(1, 2), (2, 1), (3, 0), (0, 3)]
PAIRS = (EVEN, ODD)
AXES = (("x", "y"), ("y", "x"))
PARTS = ((0, 0), (1, 0), (0, 1), (1, 1))

HBM = pl.BlockSpec(memory_space=pltpu.HBM)
VMEM = pl.BlockSpec(memory_space=pltpu.VMEM)
SMEM = pl.BlockSpec(memory_space=pltpu.SMEM)


def f32(value):
    return value.astype(jnp.float32)


def bf16(value):
    return value.astype(jnp.bfloat16)


def shape(*dims, dtype=jnp.bfloat16):
    return jax.ShapeDtypeStruct(dims, dtype)


def cost(flops, nbytes):
    return pl.CostEstimate(flops=flops, bytes_accessed=nbytes, transcendentals=0)


def offsets(i):
    sign = 1 - 2 * (i % 2)
    return (i + 2) % 4, (i + sign) % 4, (i - sign + 4) % 4, i


def blocks(g, k):
    place = {"x": offsets(lax.axis_index("x")), "y": offsets(lax.axis_index("y"))}
    first, second = AXES[g]
    one = place[first][k]
    far, near, back, own = place[second]
    result = []
    for two in (near, far, back, own):
        at = {first: one, second: two}
        result.append(at["y"] * 4 + at["x"])
    return result


def change_of(g, k, dg_ref, xt_ref, lag_ref, ss_ref, outs):
    rows = [pl.multiple_of(b * BLK, 32) for b in blocks(g, k)]
    lhs = jnp.concatenate([xt_ref[pl.ds(row, BLK), :] for row in rows], axis=0)
    cols = slice(g * HALF, (g + 1) * HALF)
    grad = jnp.dot(lhs, dg_ref[:, cols], preferred_element_type=jnp.float32)
    for m, row in enumerate(rows):
        change = grad[m * BLK : (m + 1) * BLK] * (1.0 / TOK) - f32(
            lag_ref[pl.ds(row, BLK), cols]
        )
        sq = jnp.sum((change * change).reshape(BLK // 8, 8, HALF), axis=0)
        ss_ref[...] += sum(sq[:, i * 128 : (i + 1) * 128] for i in range(5))
        out = bf16(change)
        outs[0][m] = out[:SUB]
        outs[1][m] = out[SUB:]


def first_kernel(
    x_hbm, w_hbm, up_hbm, hc_hbm, lag_hbm,
    dg_ref, xt_ref, w_ref, lag_ref, r00, r01, r10, r11, ss_ref,
    x_s, up_s, hc_s, gate_s, sem_x, sem_w, sem_a, sem_l,
):
    nw = COLS // CHUNK
    wide = [pl.ds(j * CHUNK, CHUNK) for j in range(nw)]
    get_x = pltpu.make_async_copy(x_hbm, x_s, sem_x.at[0])
    get_w = [
        pltpu.make_async_copy(w_hbm.at[:, wide[j]], w_ref.at[:, wide[j]], sem_w.at[j])
        for j in range(nw)
    ]
    get_up = pltpu.make_async_copy(up_hbm, up_s, sem_a.at[0])
    get_hc = pltpu.make_async_copy(hc_hbm, hc_s, sem_a.at[1])
    relays = blocks(0, 0) + blocks(1, 0)[:1] + blocks(1, 0)[2:]
    get_lag = []
    for b in relays + [b for k in (1, 2, 3) for i, b in enumerate(blocks(0, k)) if i != 1]:
        at = pl.ds(pl.multiple_of(b * BLK, 32), BLK)
        get_lag.append(
            pltpu.make_async_copy(lag_hbm.at[at, :], lag_ref.at[at, :], sem_l.at[len(get_lag)])
        )
    get_x.start()
    get_w[0].start()
    get_up.start()
    get_hc.start()
    for copy in get_w[1:]:
        copy.start()
    for copy in get_lag:
        copy.start()
    get_x.wait()
    for j in range(nw):
        get_w[j].wait()
        at = wide[j]
        gate = jnp.dot(x_s[...], w_ref[:, at], preferred_element_type=jnp.float32)
        lo, hi = j * 768, min(D, j * 768 + 768)
        xt_ref[lo:hi, :] = x_s[:, lo:hi].T
        if j == 0:
            get_up.wait()
            get_hc.wait()
        sig = 1.0 / (1.0 + jnp.exp(-gate))
        dg_ref[:, at] = bf16(
            f32(hc_s[:, at]) * f32(up_s[:, at]) * sig * (1.0 + gate * (1.0 - sig))
        )
    ss_ref[...] = jnp.zeros_like(ss_ref)
    for copy in get_lag[:7]:
        copy.wait()
    change_of(0, 0, dg_ref, xt_ref, lag_ref, ss_ref, (r00, r01))
    change_of(1, 0, dg_ref, xt_ref, lag_ref, ss_ref, (r10, r11))
    for copy in get_lag[7:]:
        copy.wait()


PIECE = (4, SUB, HALF)


def first(x, w, up, hc, lag):
    return pl.pallas_call(
        first_kernel,
        in_specs=[HBM] * 5,
        out_specs=[VMEM] * 9,
        out_shape=[shape(TOK, COLS), shape(D, TOK), shape(D, COLS), shape(D, COLS)]
        + [shape(*PIECE)] * 4
        + [shape(8, 128, dtype=jnp.float32)],
        scratch_shapes=[
            pltpu.VMEM((TOK, D), jnp.bfloat16),
            pltpu.VMEM((TOK, COLS), jnp.bfloat16),
            pltpu.VMEM((TOK, COLS), jnp.bfloat16),
            pltpu.VMEM((8, 128), jnp.float32),
            pltpu.SemaphoreType.DMA((1,)),
            pltpu.SemaphoreType.DMA((COLS // CHUNK,)),
            pltpu.SemaphoreType.DMA((2,)),
            pltpu.SemaphoreType.DMA((16,)),
        ],
        compiler_params=pltpu.CompilerParams(vmem_limit_bytes=16 * MIB),
        cost_estimate=cost(8 * TOK * D * COLS, 1),
        name="first",
    )(*[pltpu.with_memory_space_constraint(v, pltpu.HBM) for v in (x, w, up, hc, lag)])


RESTS = tuple((g, k) for k in (1, 2, 3) for g in range(2))


def rest_kernel(dg_ref, xt_ref, lag_ref, ss_in, *outs):
    ss_ref = outs[-1]
    ss_ref[...] = ss_in[...]
    for s, (g, k) in enumerate(RESTS):
        change_of(g, k, dg_ref, xt_ref, lag_ref, ss_ref, outs[2 * s : 2 * s + 2])


def rest(dg, xt, lag, ss):
    return pl.pallas_call(
        rest_kernel,
        in_specs=[VMEM] * 4,
        out_specs=[VMEM] * 13,
        out_shape=[shape(*PIECE)] * 12 + [shape(8, 128, dtype=jnp.float32)],
        compiler_params=pltpu.CompilerParams(vmem_limit_bytes=10 * MIB),
        cost_estimate=cost(2 * TOK * D * COLS, 20_000_000),
        name="rest",
    )(dg, xt, lag, ss)


def input_part(w_ref, dg_ref, z, c):
    row = pl.multiple_of((z * 2 + c) * INB, 64)
    return lax.dot_general(
        w_ref[pl.ds(row, INB), :],
        dg_ref[...],
        (((1,), (1,)), ((), ())),
        preferred_element_type=jnp.float32,
    )


def z_order():
    z = lax.axis_index("z")
    return (z + 1) % 4, (z + 3) % 4, (z + 2) % 4, z


def away_kernel(w_ref, dg_ref, out_ref):
    c = 1 - lax.axis_index("c")
    for i, z in enumerate(z_order()):
        out_ref[i] = bf16(input_part(w_ref, dg_ref, z, c))


def mine_kernel(w_ref, dg_ref, got_ref, *outs):
    c = lax.axis_index("c")
    for i, z in enumerate(z_order()):
        outs[i][...] = bf16(input_part(w_ref, dg_ref, z, c) + f32(got_ref[i]))


def local(kernel, out_shape, *args, limit=8, flops=1_000_000, specs=None):
    single = not isinstance(out_shape, list)
    return pl.pallas_call(
        kernel,
        in_specs=specs or [VMEM] * len(args),
        out_specs=VMEM if single else [VMEM] * len(out_shape),
        out_shape=out_shape,
        compiler_params=pltpu.CompilerParams(vmem_limit_bytes=limit * MIB),
        cost_estimate=cost(flops, 1_000_000),
    )(*args)


def factor_kernel(mask_ref, total_ref, factor_ref, rms_ref):
    total = jnp.sum(total_ref[...], axis=(0, 1), keepdims=True)
    rms = jnp.sqrt(total / (D * FF) + 1e-06)
    factor = f32(mask_ref[0]) * jnp.minimum(1.0, CLIP / rms)
    factor_ref[...] = jnp.broadcast_to(factor, (8, 128))
    rms_ref[...] = jnp.broadcast_to(rms, (8, 128))


def one(ref):
    return ref[0:1, 0:1]


def mixed_kernel(own_f, *refs):
    theirs, far, relay, outs = refs[0:4], refs[4:8], refs[8:12], refs[12:16]
    for p in range(4):
        for m in range(4):
            outs[p][m] = bf16(one(own_f) * f32(far[p][m]) + one(theirs[p]) * f32(relay[p][m]))


def merged(own_f, their_f, own, near, far, m):
    return one(own_f) * f32(own[m]) + one(their_f) * f32(near[m]) + f32(far[m])


def third_kernel(own_f, *refs):
    theirs, own, near, far, outs = (refs[4 * i : 4 * i + 4] for i in range(5))
    for p, (g, h) in enumerate(PARTS):
        for m in range(2):
            outs[p][m] = bf16(merged(own_f, theirs[p], own[p], near[p], far[p], h + m))


def fourth_kernel(own_f, *refs):
    theirs, own, near, far, third, outs = (refs[4 * i : 4 * i + 4] for i in range(6))
    for p, (g, h) in enumerate(PARTS):
        value = merged(own_f, theirs[p], own[p], near[p], far[p], 2 - 2 * h)
        outs[p][0] = bf16(value + f32(third[p][1 - h]))


def final_kernel(own_f, agg_ref, *refs):
    theirs, own, near, far, third, fourth = (refs[4 * i : 4 * i + 4] for i in range(6))
    out_ref = refs[24]
    for p, (g, h) in enumerate(PARTS):
        value = merged(own_f, theirs[p], own[p], near[p], far[p], 3)
        at = (slice(h * SUB, (h + 1) * SUB), slice(g * HALF, (g + 1) * HALF))
        out_ref[at] = agg_ref[at] + (value + f32(third[p][h]) + f32(fourth[p][0]))


def inputs_kernel(mine_ref, a_ref, b_ref, c_ref, out_ref):
    out_ref[...] = bf16(f32(mine_ref[...]) + f32(a_ref[...]) + f32(b_ref[...]) + f32(c_ref[...]))


def swap(value, axis, pairs):
    return lax.ppermute(value, axis, pairs)


def body(tokens, gate_weight, up_act, hidden_cot, lag_grads, skip_mask, aggregate):
    dg, xt, w, lag, *relay, ss = first(
        tokens, gate_weight, up_act, hidden_cot, lag_grads[0]
    )
    got_relay = [swap(relay[2 * g + h], AXES[g][0], PAIRS[h]) for g, h in PARTS]
    *pieces, total = rest(dg, xt, lag, ss)
    piece = {}
    for s, (g, k) in enumerate(RESTS):
        for h in range(2):
            piece[g, k, h] = pieces[2 * s + h]
    got_near = [swap(piece[g, 1 + h, h], AXES[g][0], PAIRS[h]) for g, h in PARTS]
    total = total + swap(total, "c", [(0, 1), (1, 0)])
    total = total + swap(total, "z", EVEN)
    total = total + swap(total, "z", ODD)
    small = shape(8, 128, dtype=jnp.float32)
    factor, rms = local(
        factor_kernel, [small, small], skip_mask, total, specs=[SMEM, VMEM], limit=1
    )
    theirs = [swap(factor, AXES[g][0], PAIRS[h]) for g, h in PARTS]

    flops = TOK * D * COLS
    away = local(away_kernel, shape(4, INB, TOK), w, dg, flops=flops, limit=4)
    away = swap(away, "c", [(0, 1), (1, 0)])
    up1, down1, two, mine = local(
        mine_kernel, [shape(INB, TOK)] * 4, w, dg, away, flops=flops, limit=4
    )
    ring = lambda by: [(i, (i + by) % 4) for i in range(4)]
    moved = [swap(up1, "z", ring(1)), swap(down1, "z", ring(3)), swap(two, "z", ring(2))]
    inp = local(inputs_kernel, shape(INB, TOK), mine, *moved)

    mixed = local(
        mixed_kernel, [shape(*PIECE)] * 4,
        factor, *theirs, *[piece[g, 2 - h, h] for g, h in PARTS], *got_relay,
    )
    got_far = [swap(value, AXES[g][0], PAIRS[1 - h]) for (g, h), value in zip(PARTS, mixed)]
    known = [*theirs, *[piece[g, 3, h] for g, h in PARTS], *got_near, *got_far]
    third = local(third_kernel, [shape(2, SUB, HALF)] * 4, factor, *known)
    third = [swap(v, AXES[g][1], PAIRS[h]) for (g, h), v in zip(PARTS, third)]
    fourth = local(fourth_kernel, [shape(1, SUB, HALF)] * 4, factor, *known, *third)
    fourth = [swap(v, AXES[g][1], PAIRS[1 - h]) for (g, h), v in zip(PARTS, fourth)]
    new = local(
        final_kernel, shape(BLK, COLS, dtype=jnp.float32),
        factor, aggregate, *known, *third, *fourth,
    )
    return new, inp.T, rms[0, :1]


def solution(mesh):
    finer = Mesh(mesh.devices.reshape(4, 4, 4, 2), ("y", "x", "z", "c"))
    dp = ("y", "x")
    placed = (
        P(dp, None),
        P(None, TENSOR),
        P(dp, TENSOR),
        P(dp, TENSOR),
        P(dp, None, TENSOR),
        P(dp),
        P(dp, TENSOR),
    )
    return jax.shard_map(
        body,
        mesh=finer,
        in_specs=placed,
        out_specs=(P(dp, TENSOR), P(dp, TENSOR), P(dp)),
        check_vma=False,
    )
```

time: 180 us -> 122 us (0.68)
  local copies, waits for them, and re-layouts: 40.2 us -> 0.51 us
  Pallas kernels: 0 us -> 37.3 us
  starting transfers between devices: 9.25 us -> 44.9 us
  matrix products: 33.5 us -> 0 us
  other arithmetic: 18.7 us -> 0.01 us
  between operations: 16.6 us -> 1.38 us
  waiting for transfers between devices: 52.9 us -> 37.8 us
  blocking collectives: 7.7 us -> 0 us
    ppermute x0 -> x31, starting transfers between devices: none -> 44.9 us  [swap(): return lax.ppermute(value, axis, pairs)]
    ppermute x0 -> x31, waiting for transfers between devices: none -> 37.8 us  [swap(): return lax.ppermute(value, axis, pairs)]
    pallas_call x0 -> x10, Pallas kernels: none -> 37.3 us  [the longest x1 21.4 us: first(): pl.pallas_call(first_kernel, in_specs=[HBM] * 5, out_specs=[VMEM] * 9, ou...]
    dot_general x3 -> x0, matrix products: 33.5 us -> none  [the longest x1 12.2 us: body(): lax.dot_general(tokens, d_gate, (((0,), (0,)), ((), ())), preferred_eleme...]
    unnamed x15 -> x2, local copies, waits for them, and re-layouts: 30.8 us -> 0.01 us
    all_to_all x2 -> x0, waiting for transfers between devices: 26.7 us -> none  [the longest x1 22.4 us: sum_by_axis(): lax.all_to_all(nearer.astype(jnp.bfloat16), far, split_axis=0, concat_axi...]
    unnamed x2 -> x0, waiting for transfers between devices: 26.2 us -> none
    convert_element_type x1 -> x0, other arithmetic: 11.1 us -> none  [body(): sent = (factor * change).astype(jnp.bfloat16)]
  transfers between devices with their start and end apart: 3 -> 31, of which waited for: 3 -> 12; matrix products, arithmetic and copies ran while one was open for 15% -> 0% of each run, Pallas kernels for 0% -> 10%
where the time goes in v1:
time: 122 us
  starting transfers between devices  44.9 us (37%)
  waiting for transfers between devices  37.8 us (31%)
  Pallas kernels  37.3 us (31%)
  between operations  1.38 us (1%)
    ppermute x31, starting transfers between devices, swap(): return lax.ppermute(value, axis, pairs)  44.9 us
    ppermute x31, waiting for transfers between devices, swap(): return lax.ppermute(value, axis, pairs)  37.8 us
    pallas_call x1, Pallas kernels, first(): pl.pallas_call(first_kernel, in_specs=[HBM] * 5, out_specs=[VMEM] * 9, ou...  21.4 us
    pallas_call x8, Pallas kernels, local(): pl.pallas_call(kernel, in_specs=specs or [VMEM] * len(args), out_specs=VM...  11.3 us
    pallas_call x1, Pallas kernels, rest(): pl.pallas_call(rest_kernel, in_specs=[VMEM] * 4, out_specs=[VMEM] * 13, o...  4.68 us
  transfers between devices with their start and end apart: 31, of which 12 were waited for; matrix products, arithmetic and copies ran while one was open for 0% of the time, Pallas kernels for 10%

profile of v1, /device:TPU:0, one launch (start us, length us, event | category | flops | bytes accessed | tf_op | source)
XLA Modules:
  0.0 121.9 jit_solution(9352818005053247628)
XLA Ops:
  0.6 21.4 %first.1 = (bf16[512,1280]{1,0:T(8,128)(2,1)S(1)}, bf16[3584,512]{1,0:T(8,128)(2,1)S(1)}, bf16[3584,1280]{1,0:T(8,128)(2,1)S(1)}, bf16[3584,1280]{1,0:T(8,128)(2...) custom-call(bf16[512,3584]{1,0:T(8,128)(2,1)} %x_hbm.1, ...), custom_call_target="tpu_custom_call" | custom-call | flops 18790481920 | bytes 1 | tf_op jit(solution)/shard_map/first/pallas_call | solution.py:137
  22.0 2.6 %shard_map.99 = bf16[4,448,512]{2,1,0:T(8,128)(2,1)S(1)} custom-call(bf16[3584,1280]{1,0:T(8,128)(2,1)S(1)} %get-tuple-element.77.w_ref, bf16[512,1280]{1,0:T(8,128)(2,1)S(1)} %get-tuple-element.43.dg_ref), custom_call_target="tpu_custom_call" | custom-call | flops 2348810240 | bytes 1000000 | tf_op jit(solution)/shard_map/pallas_call | solution.py:211
  24.8 4.7 %rest.1 = (bf16[4,112,640]{2,1,0:T(8,128)(2,1)S(1)}, bf16[4,112,640]{2,1,0:T(8,128)(2,1)S(1)}, bf16[4,112,640]{2,1,0:T(8,128)(2,1)S(1)}, bf16[4,112,640]{2,1,0:T...) custom-call(bf16[512,1280]{1,0:T(8,128)(2,1)S(1)} %get-tuple-element, ...), custom_call_target="tpu_custom_call" | custom-call | flops 4697620480 | bytes 20000000 | tf_op jit(solution)/shard_map/rest/pallas_call | solution.py:171
  30.9 2.0 %collective-permute-start.1 = (f32[8,128]{1,0:T(8,128)S(1)}, f32[8,128]{1,0:T(8,128)S(1)}, u32[]{:S(2)}, u32[]{:S(2)}) collective-permute-start(f32[8,128]{1,0:T(8,128)S(1)} %add.9), channel_id=1, source_target_pairs={{0,2},{2,0},{4,6},{6,4},{1,3},{3,1},{5,7},{7,5},{8,10},{10,8},{12,... | collective-permute-start | bytes 12296 | tf_op jit(solution)/shard_map/ppermute | solution.py:272
  33.0 1.6 %collective-permute-done.1 = f32[8,128]{1,0:T(8,128)S(1)} collective-permute-done((f32[8,128]{1,0:T(8,128)S(1)}, f32[8,128]{1,0:T(8,128)S(1)}, u32[]{:S(2)}, u32[]{:S(2)}) %collective-permute-start.1) | collective-permute-done | bytes 4128 | tf_op jit(solution)/shard_map/ppermute | solution.py:272
  34.6 4.1 %collective-permute-start.2 = (f32[8,128]{1,0:T(8,128)S(1)}, f32[8,128]{1,0:T(8,128)S(1)}, u32[]{:S(2)}, u32[]{:S(2)}) collective-permute-start(f32[8,128]{1,0:T(8,128)S(1)} %add.10), channel_id=1, source_target_pairs={{2,4},{4,2},{6,0},{0,6},{3,5},{5,3},{7,1},{1,7},{10,12},{12,10},{1... | collective-permute-start | bytes 12296 | tf_op jit(solution)/shard_map/ppermute | solution.py:272
  42.0 1.6 %collective-permute-start.4 = (f32[8,128]{1,0:T(8,128)S(1)}, f32[8,128]{1,0:T(8,128)S(1)}, u32[]{:S(2)}, u32[]{:S(2)}) collective-permute-start(f32[8,128]{1,0:T(8,128)S(1)} %get-tuple-element.48.own_f), channel_id=1, source_target_pairs={{0,32},{32,0},{64,96},{96,64},{1,33},{33,1},{65,97},{97,65},{2,34}... | collective-permute-start | bytes 12296 | tf_op jit(solution)/shard_map/ppermute | solution.py:272
  43.6 2.1 %collective-permute-start.5 = (f32[8,128]{1,0:T(8,128)S(1)}, f32[8,128]{1,0:T(8,128)S(1)}, u32[]{:S(2)}, u32[]{:S(2)}) collective-permute-start(f32[8,128]{1,0:T(8,128)S(1)} %get-tuple-element.48.own_f), channel_id=1, source_target_pairs={{8,16},{16,8},{24,0},{0,24},{9,17},{17,9},{25,1},{1,25},{10,18},{1... | collective-permute-start | bytes 12296 | tf_op jit(solution)/shard_map/ppermute | solution.py:272
  45.7 2.2 %collective-permute-start.6 = (f32[8,128]{1,0:T(8,128)S(1)}, f32[8,128]{1,0:T(8,128)S(1)}, u32[]{:S(2)}, u32[]{:S(2)}) collective-permute-start(f32[8,128]{1,0:T(8,128)S(1)} %get-tuple-element.48.own_f), channel_id=1, source_target_pairs={{32,64},{64,32},{96,0},{0,96},{33,65},{65,33},{97,1},{1,97},{34,66... | collective-permute-start | bytes 12296 | tf_op jit(solution)/shard_map/ppermute | solution.py:272
  50.5 2.2 %collective-permute-start.14 = (bf16[4,112,640]{2,1,0:T(8,128)(2,1)S(1)}, bf16[4,112,640]{2,1,0:T(8,128)(2,1)S(1)}, u32[]{:S(2)}, u32[]{:S(2)}) collective-permute-start(bf16[4,112,640]{2,1,0:T(8,128)(2,1)S(1)} %get-tuple-element.64), channel_id=1, source_target_pairs={{32,64},{64,32},{96,0},{0,96},{33,65},{65,33},{97,1},{1,97},{34,66... | collective-permute-start | bytes 1720328 | tf_op jit(solution)/shard_map/ppermute | solution.py:272
  52.7 7.5 %collective-permute-done.11.refs_8_ = bf16[4,112,640]{2,1,0:T(8,128)(2,1)S(1)} collective-permute-done((bf16[4,112,640]{2,1,0:T(8,128)(2,1)S(1)}, bf16[4,112,640]{2,1,0:T(8,128)(2,1)S(1)}, u32[]{:S(2)}, u32[]{:S(2)}) %collective-permute-start.11) | collective-permute-done | bytes 573472 | tf_op jit(solution)/shard_map/ppermute | solution.py:272
  63.2 2.5 %collective-permute-done.14.refs_11_ = bf16[4,112,640]{2,1,0:T(8,128)(2,1)S(1)} collective-permute-done((bf16[4,112,640]{2,1,0:T(8,128)(2,1)S(1)}, bf16[4,112,640]{2,1,0:T(8,128)(2,1)S(1)}, u32[]{:S(2)}, u32[]{:S(2)}) %collective-permute-start.14) | collective-permute-done | bytes 573472 | tf_op jit(solution)/shard_map/ppermute | solution.py:272
  65.7 2.7 %collective-permute-start.9 = (bf16[4,112,640]{2,1,0:T(8,128)(2,1)S(1)}, bf16[4,112,640]{2,1,0:T(8,128)(2,1)S(1)}, u32[]{:S(2)}, u32[]{:S(2)}) collective-permute-start(bf16[4,112,640]{2,1,0:T(8,128)(2,1)S(1)} %get-tuple-element.55), channel_id=1, source_target_pairs={{8,16},{16,8},{24,0},{0,24},{9,17},{17,9},{25,1},{1,25},{10,18},{1... | collective-permute-start | bytes 1720328 | tf_op jit(solution)/shard_map/ppermute | solution.py:272
  69.9 5.3 %collective-permute-done.10.refs_11_ = bf16[4,112,640]{2,1,0:T(8,128)(2,1)S(1)} collective-permute-done((bf16[4,112,640]{2,1,0:T(8,128)(2,1)S(1)}, bf16[4,112,640]{2,1,0:T(8,128)(2,1)S(1)}, u32[]{:S(2)}, u32[]{:S(2)}) %collective-permute-start.10) | collective-permute-done | bytes 573472 | tf_op jit(solution)/shard_map/ppermute | solution.py:272
  75.2 1.9 %collective-permute-start.15 = (bf16[4,112,640]{2,1,0:T(8,128)(2,1)S(1)}, bf16[4,112,640]{2,1,0:T(8,128)(2,1)S(1)}, u32[]{:S(2)}, u32[]{:S(2)}) collective-permute-start(bf16[4,112,640]{2,1,0:T(8,128)(2,1)S(1)} %get-tuple-element.65), channel_id=1, source_target_pairs={{8,16},{16,8},{24,0},{0,24},{9,17},{17,9},{25,1},{1,25},{10,18},{1... | collective-permute-start | bytes 1720328 | tf_op jit(solution)/shard_map/ppermute | solution.py:272
  79.7 9.3 %collective-permute-done.15.refs_12_ = bf16[4,112,640]{2,1,0:T(8,128)(2,1)S(1)} collective-permute-done((bf16[4,112,640]{2,1,0:T(8,128)(2,1)S(1)}, bf16[4,112,640]{2,1,0:T(8,128)(2,1)S(1)}, u32[]{:S(2)}, u32[]{:S(2)}) %collective-permute-start.15) | collective-permute-done | bytes 573472 | tf_op jit(solution)/shard_map/ppermute | solution.py:272
  91.1 1.9 %collective-permute-start.20 = (bf16[2,112,640]{2,1,0:T(8,128)(2,1)S(1)}, bf16[2,112,640]{2,1,0:T(8,128)(2,1)S(1)}, u32[]{:S(2)}, u32[]{:S(2)}) collective-permute-start(bf16[2,112,640]{2,1,0:T(8,128)(2,1)S(1)} %get-tuple-element.70), channel_id=1, source_target_pairs={{0,8},{8,0},{16,24},{24,16},{1,9},{9,1},{17,25},{25,17},{2,10},{10... | collective-permute-start | bytes 860168 | tf_op jit(solution)/shard_map/ppermute | solution.py:272
  93.0 2.2 %collective-permute-start.21 = (bf16[2,112,640]{2,1,0:T(8,128)(2,1)S(1)}, bf16[2,112,640]{2,1,0:T(8,128)(2,1)S(1)}, u32[]{:S(2)}, u32[]{:S(2)}) collective-permute-start(bf16[2,112,640]{2,1,0:T(8,128)(2,1)S(1)} %get-tuple-element.71), channel_id=1, source_target_pairs={{32,64},{64,32},{96,0},{0,96},{33,65},{65,33},{97,1},{1,97},{34,66... | collective-permute-start | bytes 860168 | tf_op jit(solution)/shard_map/ppermute | solution.py:272
  95.2 2.0 %collective-permute-start.22 = (bf16[2,112,640]{2,1,0:T(8,128)(2,1)S(1)}, bf16[2,112,640]{2,1,0:T(8,128)(2,1)S(1)}, u32[]{:S(2)}, u32[]{:S(2)}) collective-permute-start(bf16[2,112,640]{2,1,0:T(8,128)(2,1)S(1)} %get-tuple-element.72), channel_id=1, source_target_pairs={{8,16},{16,8},{24,0},{0,24},{9,17},{17,9},{25,1},{1,25},{10,18},{1... | collective-permute-start | bytes 860168 | tf_op jit(solution)/shard_map/ppermute | solution.py:272
  97.2 2.6 %shard_map.100 = (bf16[448,512]{1,0:T(8,128)(2,1)S(1)}, bf16[448,512]{1,0:T(8,128)(2,1)S(1)}, bf16[448,512]{1,0:T(8,128)(2,1)S(1)}, bf16[448,512]{1,0:T(8,128)(2,1)S(1)}) custom-call(bf16[3584,1280]{1,0:T(8,128)(2,1)S(1)} %get-tuple-element.77.w_ref, bf16[512,1280]{1,0:T(8,128)(2,1)S(1)} %get-tuple-element.43.dg_ref, ...), custom_call_target="tpu_custom_call" | custom-call | flops 2348810240 | bytes 1000000 | tf_op jit(solution)/shard_map/pallas_call | solution.py:211
  100.4 4.3 %collective-permute-start.29 = (bf16[448,512]{1,0:T(8,128)(2,1)S(1)}, bf16[448,512]{1,0:T(8,128)(2,1)S(1)}, u32[]{:S(2)}, u32[]{:S(2)}) collective-permute-start(bf16[448,512]{1,0:T(8,128)(2,1)S(1)} %get-tuple-element.80), channel_id=1, source_target_pairs={{0,6},{2,0},{4,2},{6,4},{1,7},{3,1},{5,3},{7,5},{8,14},{10,8},{12,... | collective-permute-start | bytes 1376264 | tf_op jit(solution)/shard_map/ppermute | solution.py:272
  108.6 4.6 %collective-permute-done.23.refs_20_ = bf16[1,112,640]{2,1,0:T(8,128)(2,1)S(1)} collective-permute-done((bf16[1,112,640]{2,1,0:T(8,128)(2,1)S(1)}, bf16[1,112,640]{2,1,0:T(8,128)(2,1)S(1)}, u32[]{:S(2)}, u32[]{:S(2)}) %collective-permute-start.23) | collective-permute-done | bytes 143392 | tf_op jit(solution)/shard_map/ppermute | solution.py:272
  115.1 3.2 %collective-permute-done.25.refs_22_ = bf16[1,112,640]{2,1,0:T(8,128)(2,1)S(1)} collective-permute-done((bf16[1,112,640]{2,1,0:T(8,128)(2,1)S(1)}, bf16[1,112,640]{2,1,0:T(8,128)(2,1)S(1)}, u32[]{:S(2)}, u32[]{:S(2)}) %collective-permute-start.25) | collective-permute-done | bytes 143392 | tf_op jit(solution)/shard_map/ppermute | solution.py:272
  119.1 1.9 %shard_map.98 = f32[224,1280]{1,0:T(8,128)} custom-call(f32[8,128]{1,0:T(8,128)S(1)} %get-tuple-element.48.own_f, f32[224,1280]{1,0:T(8,128)S(1)} %copy-done, f32[8,128]{1,0:T(8,128)S(1)} %collective-permute-done.3.refs_0_, f32[8,128]{1,0:T(8,128)S(1)} %collective-permute-done.4.refs_1_, f32[8,128]{1,0:T(8,128)S(1)} %collective-permute-done.5.refs_2_, ...), custom_call_target="tpu_custom_call" | custom-call | flops 1000000 | bytes 1000000 | tf_op jit(solution)/shard_map/pallas_call | solution.py:211
  (54 shorter events, 24.3 us)
Async XLA Ops:
  24.6 72.6 %collective-permute-start.27 = (bf16[4,448,512]{2,1,0:T(8,128)(2,1)S(1)}, bf16[4,448,512]{2,1,0:T(8,128)(2,1)S(1)}, u32[]{:S(2)}, u32[]{:S(2)}) collective-permute-start(bf16[4,448,512]{2,1,0:T(8,128)(2,1)S(1)} %shard_map.99), channel_id=1, source_target_pairs={{0,1},{1,0},{2,3},{3,2},{4,5},{5,4},{6,7},{7,6},{8,9},{9,8},{10,11... | collective-permute-start | bytes 5505032 | tf_op jit(solution)/shard_map/ppermute | solution.py:272
  40.4 7.4 %collective-permute-start.3 = (f32[8,128]{1,0:T(8,128)S(1)}, f32[8,128]{1,0:T(8,128)S(1)}, u32[]{:S(2)}, u32[]{:S(2)}) collective-permute-start(f32[8,128]{1,0:T(8,128)S(1)} %get-tuple-element.48.own_f), channel_id=1, source_target_pairs={{0,8},{8,0},{16,24},{24,16},{1,9},{9,1},{17,25},{25,17},{2,10},{10... | collective-permute-start | bytes 12296 | tf_op jit(solution)/shard_map/ppermute | solution.py:272
  42.0 6.5 %collective-permute-start.4 = (f32[8,128]{1,0:T(8,128)S(1)}, f32[8,128]{1,0:T(8,128)S(1)}, u32[]{:S(2)}, u32[]{:S(2)}) collective-permute-start(f32[8,128]{1,0:T(8,128)S(1)} %get-tuple-element.48.own_f), channel_id=1, source_target_pairs={{0,32},{32,0},{64,96},{96,64},{1,33},{33,1},{65,97},{97,65},{2,34}... | collective-permute-start | bytes 12296 | tf_op jit(solution)/shard_map/ppermute | solution.py:272
  47.8 12.4 %collective-permute-start.11 = (bf16[4,112,640]{2,1,0:T(8,128)(2,1)S(1)}, bf16[4,112,640]{2,1,0:T(8,128)(2,1)S(1)}, u32[]{:S(2)}, u32[]{:S(2)}) collective-permute-start(bf16[4,112,640]{2,1,0:T(8,128)(2,1)S(1)} %get-tuple-element.61), channel_id=1, source_target_pairs={{0,8},{8,0},{16,24},{24,16},{1,9},{9,1},{17,25},{25,17},{2,10},{10... | collective-permute-start | bytes 1720328 | tf_op jit(solution)/shard_map/ppermute | solution.py:272
  48.4 12.6 %collective-permute-start.12 = (bf16[4,112,640]{2,1,0:T(8,128)(2,1)S(1)}, bf16[4,112,640]{2,1,0:T(8,128)(2,1)S(1)}, u32[]{:S(2)}, u32[]{:S(2)}) collective-permute-start(bf16[4,112,640]{2,1,0:T(8,128)(2,1)S(1)} %get-tuple-element.62), channel_id=1, source_target_pairs={{0,32},{32,0},{64,96},{96,64},{1,33},{33,1},{65,97},{97,65},{2,34}... | collective-permute-start | bytes 1720328 | tf_op jit(solution)/shard_map/ppermute | solution.py:272
  49.1 12.8 %collective-permute-start.13 = (bf16[4,112,640]{2,1,0:T(8,128)(2,1)S(1)}, bf16[4,112,640]{2,1,0:T(8,128)(2,1)S(1)}, u32[]{:S(2)}, u32[]{:S(2)}) collective-permute-start(bf16[4,112,640]{2,1,0:T(8,128)(2,1)S(1)} %get-tuple-element.63), channel_id=1, source_target_pairs={{8,16},{16,8},{24,0},{0,24},{9,17},{17,9},{25,1},{1,25},{10,18},{1... | collective-permute-start | bytes 1720328 | tf_op jit(solution)/shard_map/ppermute | solution.py:272
  50.5 15.3 %collective-permute-start.14 = (bf16[4,112,640]{2,1,0:T(8,128)(2,1)S(1)}, bf16[4,112,640]{2,1,0:T(8,128)(2,1)S(1)}, u32[]{:S(2)}, u32[]{:S(2)}) collective-permute-start(bf16[4,112,640]{2,1,0:T(8,128)(2,1)S(1)} %get-tuple-element.64), channel_id=1, source_target_pairs={{32,64},{64,32},{96,0},{0,96},{33,65},{65,33},{97,1},{1,97},{34,66... | collective-permute-start | bytes 1720328 | tf_op jit(solution)/shard_map/ppermute | solution.py:272
  60.2 15.0 %collective-permute-start.10 = (bf16[4,112,640]{2,1,0:T(8,128)(2,1)S(1)}, bf16[4,112,640]{2,1,0:T(8,128)(2,1)S(1)}, u32[]{:S(2)}, u32[]{:S(2)}) collective-permute-start(bf16[4,112,640]{2,1,0:T(8,128)(2,1)S(1)} %get-tuple-element.56), channel_id=1, source_target_pairs={{32,64},{64,32},{96,0},{0,96},{33,65},{65,33},{97,1},{1,97},{34,66... | collective-permute-start | bytes 1720328 | tf_op jit(solution)/shard_map/ppermute | solution.py:272
  61.0 16.1 %collective-permute-start.7 = (bf16[4,112,640]{2,1,0:T(8,128)(2,1)S(1)}, bf16[4,112,640]{2,1,0:T(8,128)(2,1)S(1)}, u32[]{:S(2)}, u32[]{:S(2)}) collective-permute-start(bf16[4,112,640]{2,1,0:T(8,128)(2,1)S(1)} %get-tuple-element.53), channel_id=1, source_target_pairs={{0,8},{8,0},{16,24},{24,16},{1,9},{9,1},{17,25},{25,17},{2,10},{10... | collective-permute-start | bytes 1720328 | tf_op jit(solution)/shard_map/ppermute | solution.py:272
  62.0 16.6 %collective-permute-start.8 = (bf16[4,112,640]{2,1,0:T(8,128)(2,1)S(1)}, bf16[4,112,640]{2,1,0:T(8,128)(2,1)S(1)}, u32[]{:S(2)}, u32[]{:S(2)}) collective-permute-start(bf16[4,112,640]{2,1,0:T(8,128)(2,1)S(1)} %get-tuple-element.54), channel_id=1, source_target_pairs={{0,32},{32,0},{64,96},{96,64},{1,33},{33,1},{65,97},{97,65},{2,34}... | collective-permute-start | bytes 1720328 | tf_op jit(solution)/shard_map/ppermute | solution.py:272
  65.7 12.8 %collective-permute-start.9 = (bf16[4,112,640]{2,1,0:T(8,128)(2,1)S(1)}, bf16[4,112,640]{2,1,0:T(8,128)(2,1)S(1)}, u32[]{:S(2)}, u32[]{:S(2)}) collective-permute-start(bf16[4,112,640]{2,1,0:T(8,128)(2,1)S(1)} %get-tuple-element.55), channel_id=1, source_target_pairs={{8,16},{16,8},{24,0},{0,24},{9,17},{17,9},{25,1},{1,25},{10,18},{1... | collective-permute-start | bytes 1720328 | tf_op jit(solution)/shard_map/ppermute | solution.py:272
  75.2 13.7 %collective-permute-start.15 = (bf16[4,112,640]{2,1,0:T(8,128)(2,1)S(1)}, bf16[4,112,640]{2,1,0:T(8,128)(2,1)S(1)}, u32[]{:S(2)}, u32[]{:S(2)}) collective-permute-start(bf16[4,112,640]{2,1,0:T(8,128)(2,1)S(1)} %get-tuple-element.65), channel_id=1, source_target_pairs={{8,16},{16,8},{24,0},{0,24},{9,17},{17,9},{25,1},{1,25},{10,18},{1... | collective-permute-start | bytes 1720328 | tf_op jit(solution)/shard_map/ppermute | solution.py:272
  77.1 12.3 %collective-permute-start.16 = (bf16[4,112,640]{2,1,0:T(8,128)(2,1)S(1)}, bf16[4,112,640]{2,1,0:T(8,128)(2,1)S(1)}, u32[]{:S(2)}, u32[]{:S(2)}) collective-permute-start(bf16[4,112,640]{2,1,0:T(8,128)(2,1)S(1)} %get-tuple-element.66), channel_id=1, source_target_pairs={{32,64},{64,32},{96,0},{0,96},{33,65},{65,33},{97,1},{1,97},{34,66... | collective-permute-start | bytes 1720328 | tf_op jit(solution)/shard_map/ppermute | solution.py:272
  78.5 10.9 %collective-permute-start.17 = (bf16[4,112,640]{2,1,0:T(8,128)(2,1)S(1)}, bf16[4,112,640]{2,1,0:T(8,128)(2,1)S(1)}, u32[]{:S(2)}, u32[]{:S(2)}) collective-permute-start(bf16[4,112,640]{2,1,0:T(8,128)(2,1)S(1)} %get-tuple-element.67), channel_id=1, source_target_pairs={{0,8},{8,0},{16,24},{24,16},{1,9},{9,1},{17,25},{25,17},{2,10},{10... | collective-permute-start | bytes 1720328 | tf_op jit(solution)/shard_map/ppermute | solution.py:272
  78.5 10.9 %collective-permute-start.18 = (bf16[4,112,640]{2,1,0:T(8,128)(2,1)S(1)}, bf16[4,112,640]{2,1,0:T(8,128)(2,1)S(1)}, u32[]{:S(2)}, u32[]{:S(2)}) collective-permute-start(bf16[4,112,640]{2,1,0:T(8,128)(2,1)S(1)} %get-tuple-element.68), channel_id=1, source_target_pairs={{0,32},{32,0},{64,96},{96,64},{1,33},{33,1},{65,97},{97,65},{2,34}... | collective-permute-start | bytes 1720328 | tf_op jit(solution)/shard_map/ppermute | solution.py:272
  90.5 9.9 %collective-permute-start.19 = (bf16[2,112,640]{2,1,0:T(8,128)(2,1)S(1)}, bf16[2,112,640]{2,1,0:T(8,128)(2,1)S(1)}, u32[]{:S(2)}, u32[]{:S(2)}) collective-permute-start(bf16[2,112,640]{2,1,0:T(8,128)(2,1)S(1)} %get-tuple-element.69), channel_id=1, source_target_pairs={{0,32},{32,0},{64,96},{96,64},{1,33},{33,1},{65,97},{97,65},{2,34}... | collective-permute-start | bytes 860168 | tf_op jit(solution)/shard_map/ppermute | solution.py:272
  91.1 13.6 %collective-permute-start.20 = (bf16[2,112,640]{2,1,0:T(8,128)(2,1)S(1)}, bf16[2,112,640]{2,1,0:T(8,128)(2,1)S(1)}, u32[]{:S(2)}, u32[]{:S(2)}) collective-permute-start(bf16[2,112,640]{2,1,0:T(8,128)(2,1)S(1)} %get-tuple-element.70), channel_id=1, source_target_pairs={{0,8},{8,0},{16,24},{24,16},{1,9},{9,1},{17,25},{25,17},{2,10},{10... | collective-permute-start | bytes 860168 | tf_op jit(solution)/shard_map/ppermute | solution.py:272
  93.0 13.1 %collective-permute-start.21 = (bf16[2,112,640]{2,1,0:T(8,128)(2,1)S(1)}, bf16[2,112,640]{2,1,0:T(8,128)(2,1)S(1)}, u32[]{:S(2)}, u32[]{:S(2)}) collective-permute-start(bf16[2,112,640]{2,1,0:T(8,128)(2,1)S(1)} %get-tuple-element.71), channel_id=1, source_target_pairs={{32,64},{64,32},{96,0},{0,96},{33,65},{65,33},{97,1},{1,97},{34,66... | collective-permute-start | bytes 860168 | tf_op jit(solution)/shard_map/ppermute | solution.py:272
  95.2 11.0 %collective-permute-start.22 = (bf16[2,112,640]{2,1,0:T(8,128)(2,1)S(1)}, bf16[2,112,640]{2,1,0:T(8,128)(2,1)S(1)}, u32[]{:S(2)}, u32[]{:S(2)}) collective-permute-start(bf16[2,112,640]{2,1,0:T(8,128)(2,1)S(1)} %get-tuple-element.72), channel_id=1, source_target_pairs={{8,16},{16,8},{24,0},{0,24},{9,17},{17,9},{25,1},{1,25},{10,18},{1... | collective-permute-start | bytes 860168 | tf_op jit(solution)/shard_map/ppermute | solution.py:272
  99.8 21.1 %collective-permute-start.28 = (bf16[448,512]{1,0:T(8,128)(2,1)S(1)}, bf16[448,512]{1,0:T(8,128)(2,1)S(1)}, u32[]{:S(2)}, u32[]{:S(2)}) collective-permute-start(bf16[448,512]{1,0:T(8,128)(2,1)S(1)} %get-tuple-element.79), channel_id=1, source_target_pairs={{0,2},{2,4},{4,6},{6,0},{1,3},{3,5},{5,7},{7,1},{8,10},{10,12},{12... | collective-permute-start | bytes 1376264 | tf_op jit(solution)/shard_map/ppermute | solution.py:272
  100.4 20.5 %collective-permute-start.29 = (bf16[448,512]{1,0:T(8,128)(2,1)S(1)}, bf16[448,512]{1,0:T(8,128)(2,1)S(1)}, u32[]{:S(2)}, u32[]{:S(2)}) collective-permute-start(bf16[448,512]{1,0:T(8,128)(2,1)S(1)} %get-tuple-element.80), channel_id=1, source_target_pairs={{0,6},{2,0},{4,2},{6,4},{1,7},{3,1},{5,3},{7,5},{8,14},{10,8},{12,... | collective-permute-start | bytes 1376264 | tf_op jit(solution)/shard_map/ppermute | solution.py:272
  104.7 16.3 %collective-permute-start.30 = (bf16[448,512]{1,0:T(8,128)(2,1)S(1)}, bf16[448,512]{1,0:T(8,128)(2,1)S(1)}, u32[]{:S(2)}, u32[]{:S(2)}) collective-permute-start(bf16[448,512]{1,0:T(8,128)(2,1)S(1)} %get-tuple-element.81), channel_id=1, source_target_pairs={{0,4},{2,6},{4,0},{6,2},{1,5},{3,7},{5,1},{7,3},{8,12},{10,14},{12... | collective-permute-start | bytes 1376264 | tf_op jit(solution)/shard_map/ppermute | solution.py:272
  106.8 6.4 %collective-permute-start.23 = (bf16[1,112,640]{2,1,0:T(8,128)(2,1)S(1)}, bf16[1,112,640]{2,1,0:T(8,128)(2,1)S(1)}, u32[]{:S(2)}, u32[]{:S(2)}) collective-permute-start(bf16[1,112,640]{2,1,0:T(8,128)(2,1)S(1)} %get-tuple-element.73), channel_id=1, source_target_pairs={{32,64},{64,32},{96,0},{0,96},{33,65},{65,33},{97,1},{1,97},{34,66... | collective-permute-start | bytes 430088 | tf_op jit(solution)/shard_map/ppermute | solution.py:272
  107.6 6.3 %collective-permute-start.24 = (bf16[1,112,640]{2,1,0:T(8,128)(2,1)S(1)}, bf16[1,112,640]{2,1,0:T(8,128)(2,1)S(1)}, u32[]{:S(2)}, u32[]{:S(2)}) collective-permute-start(bf16[1,112,640]{2,1,0:T(8,128)(2,1)S(1)} %get-tuple-element.74), channel_id=1, source_target_pairs={{8,16},{16,8},{24,0},{0,24},{9,17},{17,9},{25,1},{1,25},{10,18},{1... | collective-permute-start | bytes 430088 | tf_op jit(solution)/shard_map/ppermute | solution.py:272
  (8 other events, 45.7 us)
